TPU v7x, 1024 devices: a whole 8x8x8 slice. The times are simulated.
1024 devices in a mesh: theta: 64 (over x_hi, z, core), band: 16 (over y, x_lo).
Axes of the slice: x: 8 (x_hi: 4, x_lo: 2; x = x_hi * 2 + x_lo), y: 8, z: 8, core: 2. Of those that a mesh axis runs over, the one named last changes fastest.
Arguments:
- basis: float32 [4, 5, 16, 8192], P(None, None, 'band', 'theta'), may hold values from -8 to 8
- jac_block: float32 [5, 5, 16, 8192], P(None, None, 'band', 'theta'), may hold values from -3 to 3
- face_coef: float32 [4, 5, 16, 8192], P(None, None, 'band', 'theta'), may hold values from 0.1 to 1.1
- panel_inverse: bfloat16 [16, 128, 320, 640], P('band', 'theta'), may hold values from -0.2 to 1.2
- rotor_offset: int32 [1], replicated, may hold values from 4032 to 4159
Outputs:
- precond: float32 [5, 16, 8192], P(None, 'band', 'theta')
- v_next: float32 [5, 16, 8192], P(None, 'band', 'theta')
- hess: float32 [5], replicated
All inputs are finite; a program needn't handle non-finite values.
Results may differ from a plain program's by a relative error of at most 0.0029.
Values may be sent and summed in bfloat16 or wider, within the bound.
A program may use at most 32 MiB of HBM per device.

v0:
```python
import jax
import jax.numpy as jnp
from jax import lax
from jax.sharding import Mesh
from jax.sharding import PartitionSpec as P

THETA = ("theta_0", "theta_1", "theta_2")
BAND = ("band_0", "band_1")
THETA_BAND = ("theta_0", "theta_1", "theta_2", "band_0", "band_1")


def extended_2(x, sides, width):
    for axis, dim in sides:
        devices, length = (lax.axis_size(axis), x.shape[dim])
        up = [(i, (i + 1) % devices) for i in range(devices)]
        down = [(j, i) for i, j in up]
        last = lax.slice_in_dim(x, length - width, length, axis=dim)
        first = lax.slice_in_dim(x, 0, width, axis=dim)
        before = lax.ppermute(last, axis, up)
        after = lax.ppermute(first, axis, down)
        x = jnp.concatenate([before, x, after], axis=dim)
    return x


def padded_2(x, sides, width):
    edges = {}
    for axis, dim in sides:
        devices, length = (lax.axis_size(axis), x.shape[dim])
        up = [(i, (i + 1) % devices) for i in range(devices)]
        last = lax.slice_in_dim(x, length - width, length, axis=dim)
        first = lax.slice_in_dim(x, 0, width, axis=dim)
        edges[dim] = (
            lax.ppermute(last, axis, up),
            lax.ppermute(first, axis, [(b, a) for a, b in up]),
        )
    done = []
    for _, dim in sides:
        low, high = edges[dim]
        around = [(width, width) if d in done else (0, 0) for d in range(x.ndim)]
        x = jnp.concatenate([jnp.pad(low, around), x, jnp.pad(high, around)], axis=dim)
        done.append(dim)
    return x


def passed_along(block, axis, distance):
    devices = range(lax.axis_size(axis))
    route = [((i - distance) % len(devices), i) for i in devices]
    return lax.ppermute(block, axis, route)


def one_axis_at_a_time(x, axes):
    for axis in axes:
        x = lax.psum(x, axis)
    return x


def on_device(basis, jac_block, face_coef, panel_inverse, rotor_offset):
    ncomp = basis.shape[1]
    rows_here = basis.shape[2]
    width = basis.shape[3]
    half_width = width // 2
    theta_count = lax.axis_size(THETA)
    band_count = lax.axis_size(BAND)
    cycle_cells = width * theta_count
    total = ncomp * rows_here * band_count * cycle_cells
    band_idx = lax.axis_index(BAND)
    resid16 = basis[-1].astype(jnp.bfloat16)
    extended = extended_2(resid16, ((THETA, 2),), half_width)
    panels = (
        extended.reshape(ncomp, rows_here, 2, width)
        .transpose(1, 2, 0, 3)
        .reshape(rows_here, 2, ncomp * width)
    )
    owned = jnp.einsum("bpij,bpj->bpi", panel_inverse, panels, preferred_element_type=jnp.float32)
    precond = (
        owned.reshape(rows_here, 2, ncomp, half_width)
        .transpose(2, 0, 1, 3)
        .reshape(ncomp, rows_here, width)
    )
    padded = padded_2(precond, ((BAND, 1), (THETA, 2)), 1)
    low_row = padded[:, 0, 1:-1]
    up_row = padded[:, -1, 1:-1]
    offset = rotor_offset[0]
    stacked = jnp.stack([up_row, low_row])
    following = passed_along(stacked, THETA, -1)
    paired = jnp.concatenate([stacked, following], axis=2)
    amounts = jnp.stack([offset % cycle_cells, (cycle_cells - offset) % cycle_cells])
    sectors = amounts // width
    within = amounts % width
    for level in range((theta_count - 1).bit_length()):
        moved = passed_along(paired, THETA, -(1 << level))
        taken = sectors // (1 << level) % 2 == 1
        paired = jnp.where(taken[:, None, None], moved, paired)
    up_shift = lax.dynamic_slice_in_dim(paired[0], within[0], width, 1)
    low_shift = lax.dynamic_slice_in_dim(paired[1], within[1], width, 1)
    middle = band_count // 2
    zero_line = jnp.zeros_like(low_row)
    lower_first = jnp.where(
        band_idx == 0, zero_line, jnp.where(band_idx == middle, low_shift, low_row)
    )
    upper_last = jnp.where(
        band_idx == band_count - 1, zero_line, jnp.where(band_idx == middle - 1, up_shift, up_row)
    )
    inner = padded[:, :, 1:-1]
    band_minus = jnp.concatenate([lower_first[:, None], inner[:, 1:rows_here]], axis=1)
    band_plus = jnp.concatenate([inner[:, 2 : rows_here + 1], upper_last[:, None]], axis=1)
    theta_minus = padded[:, 1:-1, :width]
    theta_plus = padded[:, 1:-1, 2:]
    image = 6.0 * precond + jnp.sum(jac_block * precond[None], axis=1)
    image = image - (
        face_coef[0] * theta_minus
        + face_coef[1] * theta_plus
        + face_coef[2] * band_minus
        + face_coef[3] * band_plus
    )
    local_proj = jnp.sum(basis * image[None], axis=(1, 2, 3))
    local_gram = jnp.einsum("kabc,labc->kl", basis, basis, precision=lax.Precision.HIGHEST)
    summed, image_squares, gram = (
        one_axis_at_a_time(local_proj, THETA_BAND),
        one_axis_at_a_time(jnp.sum(image * image), THETA_BAND),
        one_axis_at_a_time(local_gram, THETA_BAND),
    )
    proj = summed / total
    gram = gram / total
    ortho = image - jnp.sum(proj[:, None, None, None] * basis, axis=0)
    squares = (
        image_squares / total
        - 2.0 * jnp.sum(proj * proj)
        + jnp.sum(proj[:, None] * gram * proj[None, :])
    )
    hnorm = jnp.sqrt(squares + 1e-06)
    v_next = ortho / hnorm
    hess = jnp.concatenate([proj, hnorm[None]])
    return (precond, v_next, hess)


def solution(mesh):
    finer = Mesh(
        mesh.devices.reshape(4, 8, 2, 8, 2), ("theta_0", "theta_1", "theta_2", "band_0", "band_1")
    )
    in_specs = (
        P(None, None, BAND, THETA),
        P(None, None, BAND, THETA),
        P(None, None, BAND, THETA),
        P(BAND, THETA, None, None),
        P(),
    )
    out_specs = (P(None, BAND, THETA), P(None, BAND, THETA), P())
    return jax.shard_map(
        on_device, mesh=finer, in_specs=in_specs, out_specs=out_specs, check_vma=False
    )
```

profile of v0, /device:TPU:16, one launch (start us, length us, event | category | flops | bytes accessed | tf_op | source)
XLA Modules:
  0.0 166.0 jit_solution(14930861304673503352)
XLA Ops:
  0.6 0.8 slice.85
  1.4 0.1 fusion.26
  1.5 19.9 %collective-permute-start.1 = (bf16[5,1,64]{2,0,1:T(8,128)(2,1)S(1)}, bf16[5,1,64]{2,0,1:T(8,128)(2,1)S(1)}, u32[]{:S(2)}, u32[]{:S(2)}) collective-permute-start(bf16[5,1,64]{2,0,1:T(8,128)(2,1)S(1)} %get-tuple-element.29), channel_id=1, source_target_pairs={{16,0},{32,16},{48,32},{64,48},{80,64},{96,80},{112,96},{128,112},... | collective-permute-start | bytes 1928 | tf_op jit(solution)/shard_map/ppermute | solution.py:20
  21.4 1.9 %collective-permute-start = (bf16[5,1,64]{2,0,1:T(8,128)(2,1)S(1)}, bf16[5,1,64]{2,0,1:T(8,128)(2,1)S(1)}, u32[]{:S(2)}, u32[]{:S(2)}) collective-permute-start(bf16[5,1,64]{2,0,1:T(8,128)(2,1)S(1)} %get-tuple-element.28), channel_id=1, source_target_pairs={{0,16},{16,32},{32,48},{48,64},{64,80},{80,96},{96,112},{112,128},... | collective-permute-start | bytes 1928 | tf_op jit(solution)/shard_map/ppermute | solution.py:19
  24.0 6.5 %collective-permute-done = bf16[5,1,64]{2,0,1:T(8,128)(2,1)S(1)} collective-permute-done((bf16[5,1,64]{2,0,1:T(8,128)(2,1)S(1)}, bf16[5,1,64]{2,0,1:T(8,128)(2,1)S(1)}, u32[]{:S(2)}, u32[]{:S(2)}) %collective-permute-start) | collective-permute-done | bytes 672 | tf_op jit(solution)/shard_map/ppermute | solution.py:19
  30.5 0.1 pad_maximum_fusion.2
  30.6 0.3 fusion
  31.0 0.1 reshape.462
  31.1 0.1 reshape.463
  31.1 2.3 %collective-permute-start.4 = (f32[5,1,128]{2,1,0:T(1,128)S(1)}, f32[5,1,128]{2,1,0:T(1,128)S(1)}, u32[]{:S(2)}, u32[]{:S(2)}) collective-permute-start(f32[5,1,128]{2,1,0:T(1,128)S(1)} %reshape.463), channel_id=1, source_target_pairs={{1,0},{2,1},{3,2},{4,3},{5,4},{6,5},{7,6},{8,7},{9,8},{10,9},{11,1... | collective-permute-start | bytes 7688 | tf_op jit(solution)/shard_map/ppermute | solution.py:34
  33.4 3.6 %collective-permute-start.3 = (f32[5,1,128]{2,1,0:T(1,128)S(1)}, f32[5,1,128]{2,1,0:T(1,128)S(1)}, u32[]{:S(2)}, u32[]{:S(2)}) collective-permute-start(f32[5,1,128]{2,1,0:T(1,128)S(1)} %reshape.463), channel_id=1, source_target_pairs={{0,1},{1,2},{2,3},{3,4},{4,5},{5,6},{6,7},{7,8},{8,9},{9,10},{10,1... | collective-permute-start | bytes 7688 | tf_op jit(solution)/shard_map/ppermute | solution.py:33
  37.0 0.1 and_select_fusion
  37.1 2.7 %collective-permute-done.3 = f32[5,1,128]{2,1,0:T(1,128)S(1)} collective-permute-done((f32[5,1,128]{2,1,0:T(1,128)S(1)}, f32[5,1,128]{2,1,0:T(1,128)S(1)}, u32[]{:S(2)}, u32[]{:S(2)}) %collective-permute-start.3) | collective-permute-done | bytes 2592 | tf_op jit(solution)/shard_map/ppermute | solution.py:33
  39.8 1.9 %collective-permute-start.6 = (f32[2,5,128]{2,0,1:T(2,128)S(1)}, f32[2,5,128]{2,0,1:T(2,128)S(1)}, u32[]{:S(2)}, u32[]{:S(2)}) collective-permute-start(f32[2,5,128]{2,0,1:T(2,128)S(1)} %pad_maximum_fusion.1), channel_id=1, source_target_pairs={{16,0},{32,16},{48,32},{64,48},{80,64},{96,80},{112,96},{128,112},... | collective-permute-start | bytes 15368 | tf_op jit(solution)/shard_map/ppermute | solution.py:48
  41.8 0.1 fusion.13
  41.9 1.2 collective-permute-done.6
  43.1 7.8 %collective-permute-start.7 = (f32[2,5,256]{2,0,1:T(2,128)S(1)}, f32[2,5,256]{2,0,1:T(2,128)S(1)}, u32[]{:S(2)}, u32[]{:S(2)}) collective-permute-start(f32[2,5,256]{2,0,1:T(2,128)S(1)} %pad_maximum_fusion), channel_id=1, source_target_pairs={{16,0},{32,16},{48,32},{64,48},{80,64},{96,80},{112,96},{128,112},... | collective-permute-start | bytes 30728 | tf_op jit(solution)/shard_map/ppermute | solution.py:48
  51.0 1.3 collective-permute-done.7
  52.3 0.1 broadcast_select_fusion
  52.4 1.9 %collective-permute-start.8 = (f32[2,5,256]{2,0,1:T(2,128)S(1)}, f32[2,5,256]{2,0,1:T(2,128)S(1)}, u32[]{:S(2)}, u32[]{:S(2)}) collective-permute-start(f32[2,5,256]{2,0,1:T(2,128)S(1)} %broadcast_select_fusion), channel_id=1, source_target_pairs={{32,0},{48,16},{64,32},{80,48},{96,64},{112,80},{128,96},{144,112}... | collective-permute-start | bytes 30728 | tf_op jit(solution)/shard_map/ppermute | solution.py:48
  54.3 3.6 %collective-permute-done.8 = f32[2,5,256]{2,0,1:T(2,128)S(1)} collective-permute-done((f32[2,5,256]{2,0,1:T(2,128)S(1)}, f32[2,5,256]{2,0,1:T(2,128)S(1)}, u32[]{:S(2)}, u32[]{:S(2)}) %collective-permute-start.8) | collective-permute-done | bytes 10272 | tf_op jit(solution)/shard_map/ppermute | solution.py:48
  57.9 0.1 broadcast_select_fusion.1
  58.0 1.9 %collective-permute-start.9 = (f32[2,5,256]{2,0,1:T(2,128)S(1)}, f32[2,5,256]{2,0,1:T(2,128)S(1)}, u32[]{:S(2)}, u32[]{:S(2)}) collective-permute-start(f32[2,5,256]{2,0,1:T(2,128)S(1)} %broadcast_select_fusion.1), channel_id=1, source_target_pairs={{64,0},{80,16},{96,32},{112,48},{128,64},{144,80},{160,96},{176,11... | collective-permute-start | bytes 30728 | tf_op jit(solution)/shard_map/ppermute | solution.py:48
  59.9 0.1 convolution_bitcast_fusion
  60.1 4.4 %collective-permute-done.9 = f32[2,5,256]{2,0,1:T(2,128)S(1)} collective-permute-done((f32[2,5,256]{2,0,1:T(2,128)S(1)}, f32[2,5,256]{2,0,1:T(2,128)S(1)}, u32[]{:S(2)}, u32[]{:S(2)}) %collective-permute-start.9) | collective-permute-done | bytes 10272 | tf_op jit(solution)/shard_map/ppermute | solution.py:48
  64.5 1.9 %collective-permute-start.10 = (f32[2,5,256]{2,0,1:T(2,128)S(1)}, f32[2,5,256]{2,0,1:T(2,128)S(1)}, u32[]{:S(2)}, u32[]{:S(2)}) collective-permute-start(f32[2,5,256]{2,0,1:T(2,128)S(1)} %broadcast_select_fusion.2), channel_id=1, source_target_pairs={{128,0},{144,16},{160,32},{176,48},{192,64},{208,80},{224,96},{240... | collective-permute-start | bytes 30728 | tf_op jit(solution)/shard_map/ppermute | solution.py:48
  66.4 0.6 fusion.27
  70.9 3.1 %collective-permute-done.10 = f32[2,5,256]{2,0,1:T(2,128)S(1)} collective-permute-done((f32[2,5,256]{2,0,1:T(2,128)S(1)}, f32[2,5,256]{2,0,1:T(2,128)S(1)}, u32[]{:S(2)}, u32[]{:S(2)}) %collective-permute-start.10) | collective-permute-done | bytes 10272 | tf_op jit(solution)/shard_map/ppermute | solution.py:48
  74.1 1.9 %collective-permute-start.11 = (f32[2,5,256]{2,0,1:T(2,128)S(1)}, f32[2,5,256]{2,0,1:T(2,128)S(1)}, u32[]{:S(2)}, u32[]{:S(2)}) collective-permute-start(f32[2,5,256]{2,0,1:T(2,128)S(1)} %broadcast_select_fusion.3), channel_id=1, source_target_pairs={{256,0},{272,16},{288,32},{304,48},{320,64},{336,80},{352,96},{368... | collective-permute-start | bytes 30728 | tf_op jit(solution)/shard_map/ppermute | solution.py:48
  76.0 0.1 fusion.25
  76.1 15.8 %collective-permute-start.5 = (f32[5,1,1]{2,1,0:T(1,128)S(1)}, f32[5,1,1]{2,1,0:T(1,128)S(1)}, u32[]{:S(2)}, u32[]{:S(2)}) collective-permute-start(f32[5,1,1]{2,1,0:T(1,128)S(1)} %get-tuple-element.27), channel_id=1, source_target_pairs={{16,0},{32,16},{48,32},{64,48},{80,64},{96,80},{112,96},{128,112},... | collective-permute-start | bytes 68 | tf_op jit(solution)/shard_map/ppermute | solution.py:34
  91.9 1.9 %collective-permute-start.2 = (f32[5,1,1]{2,1,0:T(1,128)S(1)}, f32[5,1,1]{2,1,0:T(1,128)S(1)}, u32[]{:S(2)}, u32[]{:S(2)}) collective-permute-start(f32[5,1,1]{2,1,0:T(1,128)S(1)} %get-tuple-element.26), channel_id=1, source_target_pairs={{0,16},{16,32},{32,48},{48,64},{64,80},{80,96},{96,112},{112,128},... | collective-permute-start | bytes 68 | tf_op jit(solution)/shard_map/ppermute | solution.py:33
  93.8 0.1 mul.89
  94.0 5.0 %collective-permute-start.12 = (f32[2,5,256]{2,0,1:T(2,128)S(1)}, f32[2,5,256]{2,0,1:T(2,128)S(1)}, u32[]{:S(2)}, u32[]{:S(2)}) collective-permute-start(f32[2,5,256]{2,0,1:T(2,128)S(1)} %broadcast_select_fusion.4), channel_id=1, source_target_pairs={{512,0},{528,16},{544,32},{560,48},{576,64},{592,80},{608,96},{624... | collective-permute-start | bytes 30728 | tf_op jit(solution)/shard_map/ppermute | solution.py:48
  99.1 4.4 %collective-permute-done.12 = f32[2,5,256]{2,0,1:T(2,128)S(1)} collective-permute-done((f32[2,5,256]{2,0,1:T(2,128)S(1)}, f32[2,5,256]{2,0,1:T(2,128)S(1)}, u32[]{:S(2)}, u32[]{:S(2)}) %collective-permute-start.12) | collective-permute-done | bytes 10272 | tf_op jit(solution)/shard_map/ppermute | solution.py:48
  103.6 0.7 copy-done.4
  104.3 0.7 multiply_reduce_fusion.3
  105.0 0.1 multiply_reduce_fusion.2
  105.1 12.6 %all-reduce.4 = (f32[4]{0:T(128)S(1)}, f32[]{:T(128)}, f32[4,4]{1,0:T(4,128)S(1)}) all-reduce(f32[4]{0:T(128)S(1)} %multiply_reduce_fusion.2, f32[]{:T(128)} %get-tuple-element.18, f32[4,4]{1,0:T(4,128)S(1)} %convolution_bitcast_fusion), channel_id=1, replica_groups=mesh['theta_0'=4,'theta_1'=8,'theta_2'=2,'band_0'=8,'band_1'=2] {'theta_0'}, use_global_device_ids=true, to_apply=%region_2.3 | all-reduce | flops 21 | bytes 168 | tf_op jit(solution)/shard_map/psum | solution.py:53
  117.7 14.8 %all-reduce.3 = (f32[4]{0:T(128)S(1)}, f32[]{:T(128)}, f32[4,4]{1,0:T(4,128)S(1)}) all-reduce(f32[4]{0:T(128)S(1)} %get-tuple-element.9, f32[]{:T(128)} %get-tuple-element.10, f32[4,4]{1,0:T(4,128)S(1)} %get-tuple-element.11), channel_id=1, replica_groups=mesh['theta_0'=4,'theta_1'=8,'theta_2'=2,'band_0'=8,'band_1'=2] {'theta_1'}, use_global_device_ids=true, to_apply=%region_3.4 | all-reduce | flops 21 | bytes 168 | tf_op jit(solution)/shard_map/psum | solution.py:53
  132.5 3.1 %all-reduce.6 = (f32[4]{0:T(128)S(1)}, f32[]{:T(128)}, f32[4,4]{1,0:T(4,128)S(1)}) all-reduce(f32[4]{0:T(128)S(1)} %get-tuple-element.6, f32[]{:T(128)} %get-tuple-element.7, f32[4,4]{1,0:T(4,128)S(1)} %get-tuple-element.8), channel_id=1, replica_groups=mesh['theta_0'=4,'theta_1'=8,'theta_2'=2,'band_0'=8,'band_1'=2] {'theta_2'}, use_global_device_ids=true, to_apply=%region_4.5 | all-reduce | flops 21 | bytes 168 | tf_op jit(solution)/shard_map/psum | solution.py:53
  135.6 20.3 %all-reduce.2 = (f32[4]{0:T(128)S(1)}, f32[]{:T(128)}, f32[4,4]{1,0:T(4,128)S(1)}) all-reduce(f32[4]{0:T(128)S(1)} %get-tuple-element.15, f32[]{:T(128)} %get-tuple-element.16, f32[4,4]{1,0:T(4,128)S(1)} %get-tuple-element.17), channel_id=1, replica_groups=mesh['theta_0'=4,'theta_1'=8,'theta_2'=2,'band_0'=8,'band_1'=2] {'band_0'}, use_global_device_ids=true, to_apply=%region_5.6 | all-reduce | flops 21 | bytes 168 | tf_op jit(solution)/shard_map/psum | solution.py:53
  155.9 5.5 %all-reduce.5 = (f32[4]{0:T(128)S(1)}, f32[]{:T(128)}, f32[4,4]{1,0:T(4,128)S(1)}) all-reduce(f32[4]{0:T(128)S(1)} %get-tuple-element.3, f32[]{:T(128)} %get-tuple-element.4, f32[4,4]{1,0:T(4,128)S(1)} %get-tuple-element.5), channel_id=1, replica_groups=mesh['theta_0'=4,'theta_1'=8,'theta_2'=2,'band_0'=8,'band_1'=2] {'band_1'}, use_global_device_ids=true, to_apply=%region_6.7 | all-reduce | flops 21 | bytes 168 | tf_op jit(solution)/shard_map/psum | solution.py:53
  161.4 0.6 broadcast_multiply_fusion
  162.0 0.1 multiply_reduce_fusion.1
  163.4 0.7 multiply_reduce_fusion.4
  164.8 0.6 subtract_divide_fusion
  165.4 0.6 pad_maximum_fusion.7
  (29 shorter events, 0.5 us)
Async XLA Ops:
  0.6 30.0 %copy-start = (bf16[1,2,320,640]{3,2,1,0:T(8,128)(2,1)S(1)}, bf16[1,2,320,640]{3,2,1,0:T(8,128)(2,1)}, u32[]{:S(2)}) copy-start(bf16[1,2,320,640]{3,2,1,0:T(8,128)(2,1)} %param.8) | copy-start | bytes 2457604
  1.5 22.5 %collective-permute-start.1 = (bf16[5,1,64]{2,0,1:T(8,128)(2,1)S(1)}, bf16[5,1,64]{2,0,1:T(8,128)(2,1)S(1)}, u32[]{:S(2)}, u32[]{:S(2)}) collective-permute-start(bf16[5,1,64]{2,0,1:T(8,128)(2,1)S(1)} %get-tuple-element.29), channel_id=1, source_target_pairs={{16,0},{32,16},{48,32},{64,48},{80,64},{96,80},{112,96},{128,112},... | collective-permute-start | bytes 1928 | tf_op jit(solution)/shard_map/ppermute | solution.py:20
  21.4 9.1 %collective-permute-start = (bf16[5,1,64]{2,0,1:T(8,128)(2,1)S(1)}, bf16[5,1,64]{2,0,1:T(8,128)(2,1)S(1)}, u32[]{:S(2)}, u32[]{:S(2)}) collective-permute-start(bf16[5,1,64]{2,0,1:T(8,128)(2,1)S(1)} %get-tuple-element.28), channel_id=1, source_target_pairs={{0,16},{16,32},{32,48},{48,64},{64,80},{80,96},{96,112},{112,128},... | collective-permute-start | bytes 1928 | tf_op jit(solution)/shard_map/ppermute | solution.py:19
  31.1 72.4 %copy-start.2 = (f32[5,1,128]{2,1,0:T(1,128)}, f32[5,1,128]{2,1,0:T(1,128)S(1)}, u32[]{:S(2)}) copy-start(f32[5,1,128]{2,1,0:T(1,128)S(1)} %reshape.463) | copy-start | bytes 7684
  31.1 5.9 %collective-permute-start.4 = (f32[5,1,128]{2,1,0:T(1,128)S(1)}, f32[5,1,128]{2,1,0:T(1,128)S(1)}, u32[]{:S(2)}, u32[]{:S(2)}) collective-permute-start(f32[5,1,128]{2,1,0:T(1,128)S(1)} %reshape.463), channel_id=1, source_target_pairs={{1,0},{2,1},{3,2},{4,3},{5,4},{6,5},{7,6},{8,7},{9,8},{10,9},{11,1... | collective-permute-start | bytes 7688 | tf_op jit(solution)/shard_map/ppermute | solution.py:34
  33.4 6.4 %collective-permute-start.3 = (f32[5,1,128]{2,1,0:T(1,128)S(1)}, f32[5,1,128]{2,1,0:T(1,128)S(1)}, u32[]{:S(2)}, u32[]{:S(2)}) collective-permute-start(f32[5,1,128]{2,1,0:T(1,128)S(1)} %reshape.463), channel_id=1, source_target_pairs={{0,1},{1,2},{2,3},{3,4},{4,5},{5,6},{6,7},{7,8},{8,9},{9,10},{10,1... | collective-permute-start | bytes 7688 | tf_op jit(solution)/shard_map/ppermute | solution.py:33
  39.8 3.2 %collective-permute-start.6 = (f32[2,5,128]{2,0,1:T(2,128)S(1)}, f32[2,5,128]{2,0,1:T(2,128)S(1)}, u32[]{:S(2)}, u32[]{:S(2)}) collective-permute-start(f32[2,5,128]{2,0,1:T(2,128)S(1)} %pad_maximum_fusion.1), channel_id=1, source_target_pairs={{16,0},{32,16},{48,32},{64,48},{80,64},{96,80},{112,96},{128,112},... | collective-permute-start | bytes 15368 | tf_op jit(solution)/shard_map/ppermute | solution.py:48
  43.1 9.2 %collective-permute-start.7 = (f32[2,5,256]{2,0,1:T(2,128)S(1)}, f32[2,5,256]{2,0,1:T(2,128)S(1)}, u32[]{:S(2)}, u32[]{:S(2)}) collective-permute-start(f32[2,5,256]{2,0,1:T(2,128)S(1)} %pad_maximum_fusion), channel_id=1, source_target_pairs={{16,0},{32,16},{48,32},{64,48},{80,64},{96,80},{112,96},{128,112},... | collective-permute-start | bytes 30728 | tf_op jit(solution)/shard_map/ppermute | solution.py:48
  52.4 5.6 %collective-permute-start.8 = (f32[2,5,256]{2,0,1:T(2,128)S(1)}, f32[2,5,256]{2,0,1:T(2,128)S(1)}, u32[]{:S(2)}, u32[]{:S(2)}) collective-permute-start(f32[2,5,256]{2,0,1:T(2,128)S(1)} %broadcast_select_fusion), channel_id=1, source_target_pairs={{32,0},{48,16},{64,32},{80,48},{96,64},{112,80},{128,96},{144,112}... | collective-permute-start | bytes 30728 | tf_op jit(solution)/shard_map/ppermute | solution.py:48
  57.9 2.0 %copy-start.1 = (f32[4,5,1,128]{3,2,1,0:T(1,128)S(1)}, f32[4,5,1,128]{3,2,1,0:T(1,128)}, u32[]{:S(2)}) copy-start(f32[4,5,1,128]{3,2,1,0:T(1,128)} %param.5) | copy-start | bytes 30724
  58.0 6.5 %collective-permute-start.9 = (f32[2,5,256]{2,0,1:T(2,128)S(1)}, f32[2,5,256]{2,0,1:T(2,128)S(1)}, u32[]{:S(2)}, u32[]{:S(2)}) collective-permute-start(f32[2,5,256]{2,0,1:T(2,128)S(1)} %broadcast_select_fusion.1), channel_id=1, source_target_pairs={{64,0},{80,16},{96,32},{112,48},{128,64},{144,80},{160,96},{176,11... | collective-permute-start | bytes 30728 | tf_op jit(solution)/shard_map/ppermute | solution.py:48
  64.5 9.5 %collective-permute-start.10 = (f32[2,5,256]{2,0,1:T(2,128)S(1)}, f32[2,5,256]{2,0,1:T(2,128)S(1)}, u32[]{:S(2)}, u32[]{:S(2)}) collective-permute-start(f32[2,5,256]{2,0,1:T(2,128)S(1)} %broadcast_select_fusion.2), channel_id=1, source_target_pairs={{128,0},{144,16},{160,32},{176,48},{192,64},{208,80},{224,96},{240... | collective-permute-start | bytes 30728 | tf_op jit(solution)/shard_map/ppermute | solution.py:48
  74.1 19.8 %collective-permute-start.11 = (f32[2,5,256]{2,0,1:T(2,128)S(1)}, f32[2,5,256]{2,0,1:T(2,128)S(1)}, u32[]{:S(2)}, u32[]{:S(2)}) collective-permute-start(f32[2,5,256]{2,0,1:T(2,128)S(1)} %broadcast_select_fusion.3), channel_id=1, source_target_pairs={{256,0},{272,16},{288,32},{304,48},{320,64},{336,80},{352,96},{368... | collective-permute-start | bytes 30728 | tf_op jit(solution)/shard_map/ppermute | solution.py:48
  76.1 27.5 %collective-permute-start.5 = (f32[5,1,1]{2,1,0:T(1,128)S(1)}, f32[5,1,1]{2,1,0:T(1,128)S(1)}, u32[]{:S(2)}, u32[]{:S(2)}) collective-permute-start(f32[5,1,1]{2,1,0:T(1,128)S(1)} %get-tuple-element.27), channel_id=1, source_target_pairs={{16,0},{32,16},{48,32},{64,48},{80,64},{96,80},{112,96},{128,112},... | collective-permute-start | bytes 68 | tf_op jit(solution)/shard_map/ppermute | solution.py:34
  91.9 11.7 %collective-permute-start.2 = (f32[5,1,1]{2,1,0:T(1,128)S(1)}, f32[5,1,1]{2,1,0:T(1,128)S(1)}, u32[]{:S(2)}, u32[]{:S(2)}) collective-permute-start(f32[5,1,1]{2,1,0:T(1,128)S(1)} %get-tuple-element.26), channel_id=1, source_target_pairs={{0,16},{16,32},{32,48},{48,64},{64,80},{80,96},{96,112},{112,128},... | collective-permute-start | bytes 68 | tf_op jit(solution)/shard_map/ppermute | solution.py:33
  93.9 5.1 %copy-start.3 = (f32[5,5,1,128]{3,2,1,0:T(1,128)S(1)}, f32[5,5,1,128]{3,2,1,0:T(1,128)}, u32[]{:S(2)}) copy-start(f32[5,5,1,128]{3,2,1,0:T(1,128)} %param.6) | copy-start | bytes 38404
  94.0 9.5 %collective-permute-start.12 = (f32[2,5,256]{2,0,1:T(2,128)S(1)}, f32[2,5,256]{2,0,1:T(2,128)S(1)}, u32[]{:S(2)}, u32[]{:S(2)}) collective-permute-start(f32[2,5,256]{2,0,1:T(2,128)S(1)} %broadcast_select_fusion.4), channel_id=1, source_target_pairs={{512,0},{528,16},{544,32},{560,48},{576,64},{592,80},{608,96},{624... | collective-permute-start | bytes 30728 | tf_op jit(solution)/shard_map/ppermute | solution.py:48
  103.6 0.7 copy-start.4
where the time goes:
time: 167 us; the launch traced here: 166 us
  starting transfers between devices  67.9 us (41%)
  blocking collectives  56.3 us (34%)
  waiting for transfers between devices  27.3 us (16%)
  between operations  7.41 us (4%)
  other arithmetic  4.14 us (2%)
  local copies, waits for them, and re-layouts  2.48 us (1%)
    psum x5, blocking collectives, one_axis_at_a_time(): x = lax.psum(x, axis)  56.3 us
    ppermute x7, starting transfers between devices, passed_along(): return lax.ppermute(block, axis, route)  22.4 us
    ppermute x1, starting transfers between devices, extended_2(): after = lax.ppermute(first, axis, down)  19.9 us
    ppermute x2, starting transfers between devices, padded_2(): lax.ppermute(first, axis, [(b, a) for a, b in up])  18.1 us
    ppermute x7, waiting for transfers between devices, passed_along(): return lax.ppermute(block, axis, route)  18 us
    ppermute x1, waiting for transfers between devices, extended_2(): before = lax.ppermute(last, axis, up)  6.51 us
    ppermute x2, starting transfers between devices, padded_2(): lax.ppermute(last, axis, up)  5.49 us
  transfers between devices with their start and end apart: 13, of which 8 were waited for; matrix products, arithmetic and copies ran while one was open for 1% of the time, Pallas kernels for 0%

commit v1 on v0

v1 whole, which is shorter than its diff:
```python
import functools
import itertools

import jax
import jax.numpy as jnp
from jax import lax
from jax.experimental import pallas as pl
from jax.experimental.pallas import tpu as pltpu
from jax.sharding import Mesh
from jax.sharding import PartitionSpec as P

THETA = ("theta_0", "theta_1", "theta_2")
BAND = ("band_0", "band_1")
NAMES = ("theta_0", "theta_1", "theta_2", "band_0", "band_1")
MESH = pl.DeviceIdType.MESH

SIZES = {"x": 8, "y": 8, "z": 8, "c": 2}
PHASES = (("x",), ("y",), ("z", "c"))
F32 = jnp.float32
KB, NC, W = 4, 5, 128
PAIRS = [(a, b) for a in range(KB) for b in range(a, KB)]
IMG = KB + len(PAIRS)


def ring_distance(d, n):
    return min(d, n - d)


def offsets_of(axes):
    every = itertools.product(*[range(SIZES[a]) for a in axes])
    some = [o for o in every if any(o)]
    return sorted(
        some, key=lambda o: -sum(ring_distance(d, SIZES[a]) for d, a in zip(o, axes))
    )


def add_mod(v, d, n):
    if d == 0:
        return v
    s = v + d
    return jnp.where(s >= n, s - n, s)


def moved(here, axes, offset):
    t0, z, c, y, xl = here
    for a, d in zip(axes, offset):
        if d == 0:
            continue
        if a == "x":
            if d % 2:
                s = t0 + xl + d // 2
                t0 = jnp.where(s >= 4, s - 4, s)
                xl = 1 - xl
            else:
                t0 = add_mod(t0, d // 2, 4)
        elif a == "y":
            y = add_mod(y, d, 8)
        elif a == "z":
            z = add_mod(z, d, 8)
        else:
            c = 1 - c
    return (t0, z, c, y, xl)


def theta_next(here):
    t0, z, c, y, xl = here
    z1 = z + c
    over = z1 >= 8
    t1 = jnp.where(over, t0 + 1, t0)
    return (jnp.where(t1 >= 4, t1 - 4, t1), jnp.where(over, 0, z1), 1 - c, y, xl)


def theta_prev(here):
    t0, z, c, y, xl = here
    z1 = z - 1 + c
    under = z1 < 0
    t1 = jnp.where(under, t0 - 1, t0)
    return (jnp.where(t1 < 0, t1 + 4, t1), jnp.where(under, 7, z1), 1 - c, y, xl)


def band_next(here):
    t0, z, c, y, xl = here
    y1 = y + xl
    return (t0, z, c, jnp.where(y1 >= 8, y1 - 8, y1), 1 - xl)


def band_prev(here):
    t0, z, c, y, xl = here
    y1 = y - 1 + xl
    return (t0, z, c, jnp.where(y1 < 0, y1 + 8, y1), 1 - xl)


def across(here):
    t0, z, c, y, xl = here
    return (add_mod(t0, 2, 4), z, c, 7 - y, 1 - xl)


def kernel(
    total,
    basis_hbm,
    jac_hbm,
    face_hbm,
    pinv_hbm,
    off_hbm,
    precond_out,
    v_out,
    hess_out,
    basis,
    jac,
    face,
    pinv,
    off,
    mine,
    halo,
    bown,
    bhalo,
    prec,
    near,
    rotor,
    image_buf,
    load_sems,
    halo_send,
    halo_recv,
    near_send,
    near_recv,
    rotor_send,
    rotor_recv,
    *phase_refs,
):
    here = tuple(lax.axis_index(n) for n in NAMES)
    t0, z, c, y, xl = here
    band = y * 2 + xl
    at_edge = (band == 7) | (band == 8)
    left, right = theta_prev(here), theta_next(here)
    below, above = band_prev(here), band_next(here)
    opposite = across(here)
    opposite3 = (theta_prev(opposite), opposite, theta_next(opposite))

    loads = []
    zero3 = jnp.zeros((3, W), F32)
    for i in range(KB):
        loads.append((basis_hbm.at[i, :, 0, :], basis.at[i, pl.ds(0, NC), :], 0 if i == KB - 1 else 1))
    for w in range(NC):
        loads.append((jac_hbm.at[:, w, 0, :], jac.at[w, pl.ds(0, NC), :], 1))
    for d in range(4):
        loads.append((face_hbm.at[d, :, 0, :], face.at[d, pl.ds(0, NC), :], 1))
    copies = [
        pltpu.make_async_copy(src, dst, load_sems.at[k]) for k, (src, dst, _) in enumerate(loads)
    ]
    copies[KB - 1].start()
    pinv_copy = pltpu.make_async_copy(pinv_hbm.at[0], pinv, load_sems.at[len(loads)])
    pinv_copy.start()
    off_copy = pltpu.make_async_copy(off_hbm, off, load_sems.at[len(loads) + 1])
    off_copy.start()
    for k, copy in enumerate(copies):
        if k != KB - 1:
            copy.start()

    barrier = pltpu.get_barrier_semaphore()
    partners = [left, right, below, above]
    for axes in PHASES:
        partners += [moved(here, axes, o) for o in offsets_of(axes)]
    for p in partners:
        pl.semaphore_signal(barrier, inc=1, device_id=p, device_id_type=MESH)

    @pl.when(at_edge)
    def _():
        for p in opposite3:
            pl.semaphore_signal(barrier, inc=1, device_id=p, device_id_type=MESH)

    for i in range(KB):
        basis[i, NC:, :] = zero3
    for w in range(NC):
        jac[w, NC:, :] = zero3
    for d in range(4):
        face[d, NC:, :] = zero3

    lane = lax.broadcasted_iota(jnp.int32, (8, W), 1)
    row = lax.broadcasted_iota(jnp.int32, (8, W), 0)

    copies[KB - 1].wait()
    own = pltpu.roll(basis[KB - 1].astype(jnp.bfloat16).astype(F32), W // 2, 1)
    mine[...] = own

    pl.semaphore_wait(barrier, len(partners) + jnp.where(at_edge, 3, 0))
    halo_copies = []
    for k, p in enumerate((left, right)):
        copy = pltpu.make_async_remote_copy(
            mine, halo.at[1 - k], halo_send.at[k], halo_recv.at[1 - k],
            device_id=p, device_id_type=MESH,
        )
        copy.start()
        halo_copies.append(copy)

    pinv_copy.wait()
    cols = lax.broadcasted_iota(jnp.int32, (320, 640), 1) % W
    a0, a1 = pinv[0], pinv[1]
    bown[...] = jnp.where(cols < W // 2, a1, a0)
    bhalo[...] = jnp.where(cols < W // 2, a0, a1)
    xrow = lax.broadcasted_iota(jnp.int32, (W, W), 0)
    xlane = lax.broadcasted_iota(jnp.int32, (W, W), 1)
    same = (xrow < W // 2) == (xlane < W // 2)

    def spread(vec, keep):
        parts = [
            jnp.where(keep, jnp.broadcast_to(vec[u : u + 1, :], (W, W)), 0.0).astype(jnp.bfloat16)
            for u in range(NC)
        ]
        return jnp.concatenate(parts, axis=1)

    def times(mat, rhs):
        return lax.dot_general(
            mat, rhs, (((1,), (1,)), ((), ())), preferred_element_type=F32
        )

    r_own = times(bown[...], spread(own, jnp.logical_not(same)))
    pick = lax.broadcasted_iota(jnp.int32, (64, W), 0) == lax.broadcasted_iota(
        jnp.int32, (64, W), 1
    ) % 64

    def fold(r):
        return [
            jnp.sum(jnp.where(pick, r[u * 64 : (u + 1) * 64, :], 0.0), axis=0, keepdims=True)
            for u in range(NC)
        ]

    own_part = fold(r_own)

    for k, copy in enumerate(copies):
        if k != KB - 1:
            copy.wait()
    off_copy.wait()

    gram_rows = [jnp.sum(basis[a] * basis[b], axis=0, keepdims=True) for a, b in PAIRS]
    gram_rows += [jnp.zeros((1, W), F32)] * (16 - len(PAIRS))
    gram_sum = jnp.sum(jnp.concatenate(gram_rows, axis=0), axis=1, keepdims=True)
    lane16 = lax.broadcasted_iota(jnp.int32, (16, W), 1)
    row16 = lax.broadcasted_iota(jnp.int32, (16, W), 0)
    gram_line = jnp.sum(jnp.where(lane16 == row16 + KB, gram_sum, 0.0), axis=0, keepdims=True)
    gram_line = jnp.where(lane16[:1] < IMG, gram_line, 0.0)

    for k, copy in enumerate(halo_copies):
        copy.wait_recv()
    ph = jnp.where(lane < W // 2, halo[0], halo[1])
    halo_part = fold(times(bhalo[...], spread(ph, same)))
    zero1 = jnp.zeros((1, W), F32)
    pre = jnp.concatenate([a + b for a, b in zip(own_part, halo_part)] + [zero1] * 3, axis=0)
    prec[...] = pre

    near_copies = []
    for slot, p in ((3, below), (2, above), (1, left), (0, right)):
        copy = pltpu.make_async_remote_copy(
            prec, near.at[slot], near_send.at[slot], near_recv.at[slot],
            device_id=p, device_id_type=MESH,
        )
        near_copies.append(copy)
    rotor_copies = []
    for k in range(3):
        rotor_copies.append(
            pltpu.make_async_remote_copy(
                prec, rotor.at[2 - k], rotor_send.at[k], rotor_recv.at[2 - k],
                device_id=opposite3[k], device_id_type=MESH,
            )
        )

    @pl.when(at_edge)
    def _():
        for copy in rotor_copies:
            copy.start()

    for copy in near_copies:
        copy.start()

    base = 6.0 * pre
    for w in range(NC):
        base = base + jac[w] * pre[w : w + 1, :]

    for copy in near_copies:
        copy.wait_recv()
    tm = pltpu.roll(jnp.where(lane == W - 1, near[0], pre), 1, 1)
    tp = pltpu.roll(jnp.where(lane == 0, near[1], pre), W - 1, 1)
    base = base - face[0] * tm - face[1] * tp
    image_buf[...] = base
    near[2] = jnp.where(band == 0, 0.0, near[2])
    near[3] = jnp.where(band == 15, 0.0, near[3])

    @pl.when(at_edge)
    def _():
        for copy in rotor_copies:
            copy.wait_recv()
        shift = off[0] - 4032
        o = jnp.where(band == 7, shift, W - shift)
        joined = jnp.where(
            lane >= 64 + o, rotor[0], jnp.where(lane < o - 64, rotor[2], rotor[1])
        )
        turn = 64 - o
        turn = jnp.where(turn < 0, turn + W, turn)
        crossed = pltpu.roll(joined, turn, 1)
        near[2] = jnp.where(band == 8, crossed, near[2])
        near[3] = jnp.where(band == 7, crossed, near[3])

    image = image_buf[...] - face[2] * near[2] - face[3] * near[3]
    image_buf[...] = image

    late = [jnp.sum(basis[i] * image, axis=0, keepdims=True) for i in range(KB)]
    late.append(jnp.sum(image * image, axis=0, keepdims=True))
    late += [zero1] * 3
    late_sum = jnp.sum(jnp.concatenate(late, axis=0), axis=1, keepdims=True)
    want = jnp.where(row < KB, row, IMG)
    want = jnp.where(row > KB, -1, want)
    line = gram_line + jnp.sum(jnp.where(lane == want, late_sum, 0.0), axis=0, keepdims=True)

    ends = []
    for k, axes in enumerate(PHASES):
        src, slots, ssem, rsem = phase_refs[4 * k : 4 * k + 4]
        some = offsets_of(axes)
        n = len(some)
        src[...] = line
        for s, o in enumerate(some):
            pltpu.make_async_remote_copy(
                src, slots.at[pl.ds(s, 1), :], ssem, rsem,
                device_id=moved(here, axes, o), device_id_type=MESH,
            ).start()
        everything = slots.at[pl.ds(0, n), :]
        whole = pltpu.make_async_remote_copy(
            everything, everything, ssem, rsem, device_id=right, device_id_type=MESH
        )
        whole.wait_recv()
        ends.append(whole)
        line = line + jnp.sum(slots[pl.ds(0, n), :], axis=0, keepdims=True)

    line = line * (1.0 / total)
    spread16 = jnp.sum(jnp.where(lane16 == row16, line, 0.0), axis=1, keepdims=True)
    at = [jnp.broadcast_to(spread16[i : i + 1, :], (1, W)) for i in range(IMG + 1)]
    proj = at[:KB]
    gram = {pair: at[KB + k] for k, pair in enumerate(PAIRS)}
    squares = at[IMG]
    ortho = image
    for i in range(KB):
        squares = squares - 2.0 * proj[i] * proj[i]
        ortho = ortho - proj[i] * basis[i]
    for (a, b), g in gram.items():
        term = proj[a] * g * proj[b]
        squares = squares + (term if a == b else 2.0 * term)
    hnorm = jnp.sqrt(squares + 1e-06)
    v = ortho / hnorm
    for u in range(NC):
        precond_out[u] = prec[u : u + 1, :]
        v_out[u] = v[u : u + 1, :]
    hess_out[...] = jnp.where(lane[:1] < KB, line, hnorm)

    for copy in halo_copies + near_copies + ends:
        copy.wait_send()

    @pl.when(at_edge)
    def _():
        for copy in rotor_copies:
            copy.wait_send()


def on_device(basis, jac_block, face_coef, panel_inverse, rotor_offset):
    total = basis.shape[1] * basis.shape[2] * basis.shape[3] * lax.axis_size(NAMES)
    row = jax.ShapeDtypeStruct((NC, 1, W), F32)
    any_space = pl.BlockSpec(memory_space=pl.ANY)
    vmem = pl.BlockSpec(memory_space=pltpu.VMEM)
    dma = pltpu.SemaphoreType.DMA
    phase_shapes = []
    for axes in PHASES:
        n = len(offsets_of(axes))
        phase_shapes += [
            pltpu.VMEM((1, W), F32),
            pltpu.VMEM(((n + 7) // 8 * 8, W), F32),
            dma,
            dma,
        ]
    precond, v, hess = pl.pallas_call(
        functools.partial(kernel, float(total)),
        out_shape=(row, row, jax.ShapeDtypeStruct((1, W), F32)),
        in_specs=[any_space] * 5,
        out_specs=(vmem,) * 3,
        scratch_shapes=[
            pltpu.VMEM((KB, 8, W), F32),
            pltpu.VMEM((NC, 8, W), F32),
            pltpu.VMEM((4, 8, W), F32),
            pltpu.VMEM((2, 320, 640), jnp.bfloat16),
            pltpu.SMEM((1,), jnp.int32),
            pltpu.VMEM((8, W), F32),
            pltpu.VMEM((2, 8, W), F32),
            pltpu.VMEM((320, 640), jnp.bfloat16),
            pltpu.VMEM((320, 640), jnp.bfloat16),
            pltpu.VMEM((8, W), F32),
            pltpu.VMEM((4, 8, W), F32),
            pltpu.VMEM((3, 8, W), F32),
            pltpu.VMEM((8, W), F32),
            dma((15,)),
            dma((2,)),
            dma((2,)),
            dma((4,)),
            dma((4,)),
            dma((3,)),
            dma((3,)),
            *phase_shapes,
        ],
        compiler_params=pltpu.CompilerParams(collective_id=0, has_side_effects=True),
        name="schwarz_step",
    )(basis, jac_block, face_coef, panel_inverse, rotor_offset)
    return precond, v, hess[0, : KB + 1]


def solution(mesh):
    finer = Mesh(mesh.devices.reshape(4, 8, 2, 8, 2), NAMES)
    in_specs = (
        P(None, None, BAND, THETA),
        P(None, None, BAND, THETA),
        P(None, None, BAND, THETA),
        P(BAND, THETA, None, None),
        P(),
    )
    out_specs = (P(None, BAND, THETA), P(None, BAND, THETA), P())
    return jax.shard_map(
        on_device, mesh=finer, in_specs=in_specs, out_specs=out_specs, check_vma=False
    )
```

time: 167 us -> 50.9 us (0.30)
  the two profiles are of different devices: /device:TPU:16 before, /device:TPU:1 now
where the time goes in v1:
time: 50.9 us; the launch traced here: 50.7 us
  Pallas kernels  47 us (92%)
  local copies, waits for them, and re-layouts  2.36 us (5%)
  between operations  1.3 us (3%)
    pallas_call x1, Pallas kernels, on_device(): pl.pallas_call(functools.partial(kernel, float(total)), out_shape=(row, r...  47 us
    unnamed x8, local copies, waits for them, and re-layouts  1.85 us

profile of v1, /device:TPU:1, one launch (start us, length us, event | category | flops | bytes accessed | tf_op | source)
XLA Modules:
  0.0 50.7 jit_solution(5757368751709572302)
XLA Ops:
  1.3 47.0 %schwarz_step.1 = (f32[5,1,128]{2,1,0:T(1,128)}, f32[5,1,128]{2,1,0:T(1,128)}, f32[1,128]{1,0:T(1,128)}) custom-call(f32[4,5,1,128]{3,2,1,0:T(1,128)} %basis_hbm.1, f32[5,5,1,128]{3,2,1,0:T(1,128)} %jac_hbm.1, f32[4,5,1,128]{3,2,1,0:T(1,128)} %face_hbm.1, bf16[1,2,320,640]{3,2,1,0:T(8,128)(2,1)} %pinv_hbm.1, s32[1]{0:T(128)S(6)} %copy.10.off_hbm), custom_call_target="tpu_custom_call" | custom-call | tf_op jit(solution)/shard_map/schwarz_step/pallas_call | solution.py:376
  48.3 0.0 copy-start.1
  48.3 0.0 copy-start.2
  48.3 0.6 %copy-done.2 = f32[1,128]{1,0:T(1,128)S(1)} copy-done((f32[1,128]{1,0:T(1,128)S(1)}, f32[1,128]{1,0:T(1,128)}, u32[]{:S(2)}) %copy-start.2) | copy-done | bytes 536
  48.9 0.5 %slice_bitcast_fusion = f32[5]{0:T(128)} fusion(f32[1,128]{1,0:T(1,128)S(1)} %copy-done.2), kind=kLoop, calls=%fused_computation | loop fusion | bytes 40 | tf_op jit(solution)/shard_map/squeeze | solution.py:407
  49.4 0.0 copy-done.1
  49.4 0.0 copy-start
  49.4 0.6 %copy.11 = f32[5,1,128]{2,1,0:T(1,128)} copy(f32[5,1,128]{2,1,0:T(1,128)S(1)} %copy-done.1) | data formatting | bytes 5120
  50.0 0.1 copy-done
  50.1 0.6 %copy.12 = f32[5,1,128]{2,1,0:T(1,128)} copy(f32[5,1,128]{2,1,0:T(1,128)S(1)} %copy-done) | data formatting | bytes 5120
Async XLA Ops:
  48.3 1.1 %copy-start.1 = (f32[5,1,128]{2,1,0:T(1,128)S(1)}, f32[5,1,128]{2,1,0:T(1,128)}, u32[]{:S(2)}) copy-start(f32[5,1,128]{2,1,0:T(1,128)} %get-tuple-element.12) | copy-start | bytes 7684
  48.3 0.6 %copy-start.2 = (f32[1,128]{1,0:T(1,128)S(1)}, f32[1,128]{1,0:T(1,128)}, u32[]{:S(2)}) copy-start(f32[1,128]{1,0:T(1,128)} %get-tuple-element.8) | copy-start | bytes 1540
  49.4 0.7 %copy-start = (f32[5,1,128]{2,1,0:T(1,128)S(1)}, f32[5,1,128]{2,1,0:T(1,128)}, u32[]{:S(2)}) copy-start(f32[5,1,128]{2,1,0:T(1,128)} %get-tuple-element.13) | copy-start | bytes 7684

commit v2 on v1

--- a/solution.py
+++ b/solution.py
@@ -15,7 +15,7 @@
 MESH = pl.DeviceIdType.MESH
 
 SIZES = {"x": 8, "y": 8, "z": 8, "c": 2}
-PHASES = (("x",), ("y",), ("z", "c"))
+PHASES = (("x", "y"), ("z", "c"))
 F32 = jnp.float32
 KB, NC, W = 4, 5, 128
 PAIRS = [(a, b) for a in range(KB) for b in range(a, KB)]
@@ -101,23 +101,21 @@
     jac_hbm,
     face_hbm,
     pinv_hbm,
-    off_hbm,
-    precond_out,
-    v_out,
-    hess_out,
+    off,
+    image_buf,
+    prec,
+    line_out,
     basis,
     jac,
     face,
     pinv,
-    off,
     mine,
     halo,
     bown,
     bhalo,
-    prec,
     near,
     rotor,
-    image_buf,
+    met,
     load_sems,
     halo_send,
     halo_recv,
@@ -150,23 +148,20 @@
     copies[KB - 1].start()
     pinv_copy = pltpu.make_async_copy(pinv_hbm.at[0], pinv, load_sems.at[len(loads)])
     pinv_copy.start()
-    off_copy = pltpu.make_async_copy(off_hbm, off, load_sems.at[len(loads) + 1])
-    off_copy.start()
     for k, copy in enumerate(copies):
         if k != KB - 1:
             copy.start()
 
     barrier = pltpu.get_barrier_semaphore()
-    partners = [left, right, below, above]
-    for axes in PHASES:
-        partners += [moved(here, axes, o) for o in offsets_of(axes)]
+    ones = [(a, o) for a in "xyz" for o in (1, 7)]
+    steps = [moved(here, (a,), (o,)) for a, o in ones]
+    partners = [left, right, below, above] + steps
     for p in partners:
         pl.semaphore_signal(barrier, inc=1, device_id=p, device_id_type=MESH)
 
-    @pl.when(at_edge)
-    def _():
-        for p in opposite3:
-            pl.semaphore_signal(barrier, inc=1, device_id=p, device_id_type=MESH)
+    def tell(k, devices):
+        for p in devices:
+            pl.semaphore_signal(met.at[k], inc=1, device_id=p, device_id_type=MESH)
 
     for i in range(KB):
         basis[i, NC:, :] = zero3
@@ -182,7 +177,7 @@
     own = pltpu.roll(basis[KB - 1].astype(jnp.bfloat16).astype(F32), W // 2, 1)
     mine[...] = own
 
-    pl.semaphore_wait(barrier, len(partners) + jnp.where(at_edge, 3, 0))
+    pl.semaphore_wait(barrier, len(partners))
     halo_copies = []
     for k, p in enumerate((left, right)):
         copy = pltpu.make_async_remote_copy(
@@ -191,6 +186,7 @@
         )
         copy.start()
         halo_copies.append(copy)
+    tell(0, steps)
 
     pinv_copy.wait()
     cols = lax.broadcasted_iota(jnp.int32, (320, 640), 1) % W
@@ -226,10 +222,13 @@
 
     own_part = fold(r_own)
 
+    pl.semaphore_wait(met.at[0], len(steps))
+    twos = [moved(here, (a,), (2 if o == 1 else 6,)) for a, o in ones]
+    tell(1, twos)
+
     for k, copy in enumerate(copies):
         if k != KB - 1:
             copy.wait()
-    off_copy.wait()
 
     gram_rows = [jnp.sum(basis[a] * basis[b], axis=0, keepdims=True) for a, b in PAIRS]
     gram_rows += [jnp.zeros((1, W), F32)] * (16 - len(PAIRS))
@@ -263,17 +262,24 @@
             )
         )
 
+    for copy in near_copies:
+        copy.start()
+
+    pl.semaphore_wait(met.at[1], len(twos))
+    tell(2, (left, right))
+    column = [moved(here, ("y",), (d,)) for d in (4, 3, 5, 2, 6, 1, 7)]
+    tell(3, column)
+
+    base = 6.0 * pre
+    for w in range(NC):
+        base = base + jac[w] * pre[w : w + 1, :]
+
+    pl.semaphore_wait(met.at[2], 2)
+
     @pl.when(at_edge)
     def _():
         for copy in rotor_copies:
             copy.start()
-
-    for copy in near_copies:
-        copy.start()
-
-    base = 6.0 * pre
-    for w in range(NC):
-        base = base + jac[w] * pre[w : w + 1, :]
 
     for copy in near_copies:
         copy.wait_recv()
@@ -298,6 +304,8 @@
         crossed = pltpu.roll(joined, turn, 1)
         near[2] = jnp.where(band == 8, crossed, near[2])
         near[3] = jnp.where(band == 7, crossed, near[3])
+
+    pl.semaphore_wait(met.at[3], len(column))
 
     image = image_buf[...] - face[2] * near[2] - face[3] * near[3]
     image_buf[...] = image
@@ -329,13 +337,27 @@
         ends.append(whole)
         line = line + jnp.sum(slots[pl.ds(0, n), :], axis=0, keepdims=True)
 
-    line = line * (1.0 / total)
+    line_out[...] = line
+
+    for copy in halo_copies + near_copies + ends:
+        copy.wait_send()
+
+    @pl.when(at_edge)
+    def _():
+        for copy in rotor_copies:
+            copy.wait_send()
+
+
+def finish(total, image, prec, line_in, basis, precond_out, v_out, hess_out):
+    line = line_in[...] * (1.0 / total)
+    lane16 = lax.broadcasted_iota(jnp.int32, (16, W), 1)
+    row16 = lax.broadcasted_iota(jnp.int32, (16, W), 0)
     spread16 = jnp.sum(jnp.where(lane16 == row16, line, 0.0), axis=1, keepdims=True)
     at = [jnp.broadcast_to(spread16[i : i + 1, :], (1, W)) for i in range(IMG + 1)]
     proj = at[:KB]
     gram = {pair: at[KB + k] for k, pair in enumerate(PAIRS)}
     squares = at[IMG]
-    ortho = image
+    ortho = image[...]
     for i in range(KB):
         squares = squares - 2.0 * proj[i] * proj[i]
         ortho = ortho - proj[i] * basis[i]
@@ -347,21 +369,13 @@
     for u in range(NC):
         precond_out[u] = prec[u : u + 1, :]
         v_out[u] = v[u : u + 1, :]
-    hess_out[...] = jnp.where(lane[:1] < KB, line, hnorm)
-
-    for copy in halo_copies + near_copies + ends:
-        copy.wait_send()
-
-    @pl.when(at_edge)
-    def _():
-        for copy in rotor_copies:
-            copy.wait_send()
+    hess_out[...] = jnp.where(lane16[:1] < KB, line, hnorm)[0, : KB + 1]
 
 
 def on_device(basis, jac_block, face_coef, panel_inverse, rotor_offset):
     total = basis.shape[1] * basis.shape[2] * basis.shape[3] * lax.axis_size(NAMES)
     row = jax.ShapeDtypeStruct((NC, 1, W), F32)
-    any_space = pl.BlockSpec(memory_space=pl.ANY)
+    arrays = (basis, jac_block, face_coef, panel_inverse)
     vmem = pl.BlockSpec(memory_space=pltpu.VMEM)
     dma = pltpu.SemaphoreType.DMA
     phase_shapes = []
@@ -373,26 +387,30 @@
             dma,
             dma,
         ]
-    precond, v, hess = pl.pallas_call(
+    tile = jax.ShapeDtypeStruct((8, W), F32)
+    hbm = pl.BlockSpec(memory_space=pltpu.HBM)
+    image, precond, line, basis_tiles = pl.pallas_call(
         functools.partial(kernel, float(total)),
-        out_shape=(row, row, jax.ShapeDtypeStruct((1, W), F32)),
-        in_specs=[any_space] * 5,
-        out_specs=(vmem,) * 3,
+        out_shape=(
+            tile,
+            tile,
+            jax.ShapeDtypeStruct((1, W), F32),
+            jax.ShapeDtypeStruct((KB, 8, W), F32),
+        ),
+        in_specs=[hbm] * 4 + [pl.BlockSpec(memory_space=pltpu.SMEM)],
+        out_specs=(vmem,) * 4,
         scratch_shapes=[
-            pltpu.VMEM((KB, 8, W), F32),
             pltpu.VMEM((NC, 8, W), F32),
             pltpu.VMEM((4, 8, W), F32),
             pltpu.VMEM((2, 320, 640), jnp.bfloat16),
-            pltpu.SMEM((1,), jnp.int32),
             pltpu.VMEM((8, W), F32),
             pltpu.VMEM((2, 8, W), F32),
             pltpu.VMEM((320, 640), jnp.bfloat16),
             pltpu.VMEM((320, 640), jnp.bfloat16),
-            pltpu.VMEM((8, W), F32),
             pltpu.VMEM((4, 8, W), F32),
             pltpu.VMEM((3, 8, W), F32),
-            pltpu.VMEM((8, W), F32),
-            dma((15,)),
+            pltpu.SemaphoreType.REGULAR((4,)),
+            dma((14,)),
             dma((2,)),
             dma((2,)),
             dma((4,)),
@@ -401,10 +419,19 @@
             dma((3,)),
             *phase_shapes,
         ],
-        compiler_params=pltpu.CompilerParams(collective_id=0, has_side_effects=True),
+        compiler_params=pltpu.CompilerParams(
+            collective_id=0, has_side_effects=True, vmem_limit_bytes=8 << 20
+        ),
         name="schwarz_step",
-    )(basis, jac_block, face_coef, panel_inverse, rotor_offset)
-    return precond, v, hess[0, : KB + 1]
+    )(*[pltpu.with_memory_space_constraint(a, pltpu.HBM) for a in arrays], rotor_offset)
+    return pl.pallas_call(
+        functools.partial(finish, float(total)),
+        out_shape=(row, row, jax.ShapeDtypeStruct((KB + 1,), F32)),
+        in_specs=[vmem] * 4,
+        out_specs=(vmem,) * 3,
+        compiler_params=pltpu.CompilerParams(vmem_limit_bytes=4 << 20),
+        name="schwarz_finish",
+    )(image, precond, line, basis_tiles)
 
 
 def solution(mesh):

time: 50.9 us -> 47 us (0.923)
  local copies, waits for them, and re-layouts: 2.36 us -> 0 us
  Pallas kernels: 47 us -> 45.5 us
    unnamed x8 -> x0, local copies, waits for them, and re-layouts: 1.85 us -> none
    pallas_call x1 -> x2, Pallas kernels: 47 us -> 45.5 us  [the longest x1 44.8 us: on_device(): pl.pallas_call(functools.partial(kernel, float(total)), out_shape=(tile,...]
    squeeze x1 -> x0, local copies, waits for them, and re-layouts: 0.51 us -> none  [on_device(): return (precond, v, hess[0, :KB + 1])]
where the time goes in v2:
time: 47 us; the launch traced here: 46.8 us
  Pallas kernels  45.5 us (97%)
  between operations  1.29 us (3%)
    pallas_call x1, Pallas kernels, on_device(): pl.pallas_call(functools.partial(kernel, float(total)), out_shape=(tile,...  44.8 us

profile of v2, /device:TPU:1, one launch (start us, length us, event | category | flops | bytes accessed | tf_op | source)
XLA Modules:
  0.0 46.8 jit_solution(10726415902427216284)
XLA Ops:
  1.3 44.8 %schwarz_step.1 = (f32[8,128]{1,0:T(8,128)S(1)}, f32[8,128]{1,0:T(8,128)S(1)}, f32[1,128]{1,0:T(1,128)S(1)}, f32[4,8,128]{2,1,0:T(8,128)S(1)}) custom-call(f32[4,5,1,128]{3,2,1,0:T(1,128)} %basis_hbm.1, f32[5,5,1,128]{3,2,1,0:T(1,128)} %jac_hbm.1, f32[4,5,1,128]{3,2,1,0:T(1,128)} %face_hbm.1, bf16[1,2,320,640]{3,2,1,0:T(8,128)(2,1)} %pinv_hbm.1, s32[1]{0:T(128)S(6)} %copy.8.off), custom_call_target="tpu_custom_call" | custom-call | tf_op jit(solution)/shard_map/schwarz_step/pallas_call | solution.py:392
  46.1 0.7 %schwarz_finish.1 = (f32[5,1,128]{2,1,0:T(1,128)}, f32[5,1,128]{2,1,0:T(1,128)}, f32[5]{0:T(128)}) custom-call(f32[8,128]{1,0:T(8,128)S(1)} %get-tuple-element.7.image, f32[8,128]{1,0:T(8,128)S(1)} %get-tuple-element.8.prec, f32[1,128]{1,0:T(1,128)S(1)} %get-tuple-element.9.line_in, f32[4,8,128]{2,1,0:T(8,128)S(1)} %get-tuple-element.10.basis), custom_call_target="tpu_custom_call" | custom-call | tf_op jit(solution)/shard_map/schwarz_finish/pallas_call | solution.py:427

commit v3 on v2

--- a/solution.py
+++ b/solution.py
@@ -15,7 +15,7 @@
 MESH = pl.DeviceIdType.MESH
 
 SIZES = {"x": 8, "y": 8, "z": 8, "c": 2}
-PHASES = (("x", "y"), ("z", "c"))
+PHASES = (("z", "c"), ("x", "y"))
 F32 = jnp.float32
 KB, NC, W = 4, 5, 128
 PAIRS = [(a, b) for a in range(KB) for b in range(a, KB)]
@@ -111,6 +111,8 @@
     pinv,
     mine,
     halo,
+    edge_out,
+    edge_in,
     bown,
     bhalo,
     near,
@@ -119,6 +121,8 @@
     load_sems,
     halo_send,
     halo_recv,
+    edge_send,
+    edge_recv,
     near_send,
     near_recv,
     rotor_send,
@@ -129,6 +133,8 @@
     t0, z, c, y, xl = here
     band = y * 2 + xl
     at_edge = (band == 7) | (band == 8)
+    has_low = (band != 0) & (band != 8)
+    has_high = (band != 7) & (band != 15)
     left, right = theta_prev(here), theta_next(here)
     below, above = band_prev(here), band_next(here)
     opposite = across(here)
@@ -159,6 +165,11 @@
     for p in partners:
         pl.semaphore_signal(barrier, inc=1, device_id=p, device_id_type=MESH)
 
+    @pl.when(band == 7)
+    def _():
+        for p in opposite3:
+            pl.semaphore_signal(barrier, inc=1, device_id=p, device_id_type=MESH)
+
     def tell(k, devices):
         for p in devices:
             pl.semaphore_signal(met.at[k], inc=1, device_id=p, device_id_type=MESH)
@@ -173,22 +184,48 @@
     lane = lax.broadcasted_iota(jnp.int32, (8, W), 1)
     row = lax.broadcasted_iota(jnp.int32, (8, W), 0)
 
+    pl.semaphore_wait(barrier, len(partners) + jnp.where(band == 8, 3, 0))
+
+    @pl.when(band == 8)
+    def _():
+        tell(4, opposite3)
+
+    tell(0, steps)
+
     copies[KB - 1].wait()
     own = pltpu.roll(basis[KB - 1].astype(jnp.bfloat16).astype(F32), W // 2, 1)
     mine[...] = own
 
-    pl.semaphore_wait(barrier, len(partners))
-    halo_copies = []
-    for k, p in enumerate((left, right)):
-        copy = pltpu.make_async_remote_copy(
-            mine, halo.at[1 - k], halo_send.at[k], halo_recv.at[1 - k],
-            device_id=p, device_id_type=MESH,
-        )
-        copy.start()
-        halo_copies.append(copy)
-    tell(0, steps)
+    to_left = pltpu.make_async_remote_copy(
+        mine, halo.at[1], halo_send.at[0], halo_recv.at[1], device_id=left, device_id_type=MESH
+    )
+    to_right = pltpu.make_async_remote_copy(
+        mine, halo.at[0], halo_send.at[1], halo_recv.at[0], device_id=right, device_id_type=MESH
+    )
+    edge_left = pltpu.make_async_remote_copy(
+        edge_out.at[0], edge_in.at[1], edge_send.at[0], edge_recv.at[1],
+        device_id=left, device_id_type=MESH,
+    )
+    edge_right = pltpu.make_async_remote_copy(
+        edge_out.at[1], edge_in.at[0], edge_send.at[1], edge_recv.at[0],
+        device_id=right, device_id_type=MESH,
+    )
+    to_right.start()
+
+    to_left.start()
 
     pinv_copy.wait()
+
+    def rows_of(side, k):
+        some = [pinv[side, u * 64 + k : u * 64 + k + 1, :].astype(F32) for u in range(NC)]
+        return jnp.concatenate(some + [jnp.zeros((3, 640), F32)], axis=0).astype(jnp.bfloat16)
+
+    edge_out[0] = rows_of(0, 0)
+    edge_out[1] = rows_of(1, 63)
+    edge_right.start()
+
+    edge_left.start()
+
     cols = lax.broadcasted_iota(jnp.int32, (320, 640), 1) % W
     a0, a1 = pinv[0], pinv[1]
     bown[...] = jnp.where(cols < W // 2, a1, a0)
@@ -238,21 +275,29 @@
     gram_line = jnp.sum(jnp.where(lane16 == row16 + KB, gram_sum, 0.0), axis=0, keepdims=True)
     gram_line = jnp.where(lane16[:1] < IMG, gram_line, 0.0)
 
-    for k, copy in enumerate(halo_copies):
-        copy.wait_recv()
+    to_right.wait_recv()
+    to_left.wait_recv()
     ph = jnp.where(lane < W // 2, halo[0], halo[1])
     halo_part = fold(times(bhalo[...], spread(ph, same)))
     zero1 = jnp.zeros((1, W), F32)
     pre = jnp.concatenate([a + b for a, b in zip(own_part, halo_part)] + [zero1] * 3, axis=0)
     prec[...] = pre
 
-    near_copies = []
-    for slot, p in ((3, below), (2, above), (1, left), (0, right)):
-        copy = pltpu.make_async_remote_copy(
-            prec, near.at[slot], near_send.at[slot], near_recv.at[slot],
-            device_id=p, device_id_type=MESH,
-        )
-        near_copies.append(copy)
+    to_low = pltpu.make_async_remote_copy(
+        prec, near.at[1], near_send.at[0], near_recv.at[1], device_id=below, device_id_type=MESH
+    )
+    to_high = pltpu.make_async_remote_copy(
+        prec, near.at[0], near_send.at[1], near_recv.at[0], device_id=above, device_id_type=MESH
+    )
+
+    @pl.when(has_low)
+    def _():
+        to_low.start()
+
+    @pl.when(has_high)
+    def _():
+        to_high.start()
+
     rotor_copies = []
     for k in range(3):
         rotor_copies.append(
@@ -262,33 +307,54 @@
             )
         )
 
-    for copy in near_copies:
-        copy.start()
+    @pl.when(band == 7)
+    def _():
+        pl.semaphore_wait(met.at[4], 3)
+
+    @pl.when(at_edge)
+    def _():
+        for copy in rotor_copies:
+            copy.start()
 
     pl.semaphore_wait(met.at[1], len(twos))
-    tell(2, (left, right))
+    tell(2, [(t0, z, 1 - c, y, xl)])
     column = [moved(here, ("y",), (d,)) for d in (4, 3, 5, 2, 6, 1, 7)]
     tell(3, column)
 
-    base = 6.0 * pre
+    edge_right.wait_recv()
+    edge_left.wait_recv()
+    panel0 = jnp.where(lane < W // 2, ph, own)
+    panel1 = jnp.where(lane < W // 2, own, ph)
+
+    def edge_of(side, panel):
+        rows = edge_in[side].astype(F32)
+        total_row = rows[:, :W] * panel[0:1, :]
+        for u in range(1, NC):
+            total_row = total_row + rows[:, u * W : (u + 1) * W] * panel[u : u + 1, :]
+        return jnp.sum(total_row, axis=1, keepdims=True)
+
+    tm = jnp.where(lane == 0, edge_of(0, panel0), pltpu.roll(pre, 1, 1))
+    tp = jnp.where(lane == W - 1, edge_of(1, panel1), pltpu.roll(pre, W - 1, 1))
+    base = 6.0 * pre - face[0] * tm - face[1] * tp
     for w in range(NC):
         base = base + jac[w] * pre[w : w + 1, :]
-
-    pl.semaphore_wait(met.at[2], 2)
-
-    @pl.when(at_edge)
-    def _():
-        for copy in rotor_copies:
-            copy.start()
-
-    for copy in near_copies:
-        copy.wait_recv()
-    tm = pltpu.roll(jnp.where(lane == W - 1, near[0], pre), 1, 1)
-    tp = pltpu.roll(jnp.where(lane == 0, near[1], pre), W - 1, 1)
-    base = base - face[0] * tm - face[1] * tp
     image_buf[...] = base
-    near[2] = jnp.where(band == 0, 0.0, near[2])
-    near[3] = jnp.where(band == 15, 0.0, near[3])
+
+    @pl.when(has_low)
+    def _():
+        to_high.wait_recv()
+
+    @pl.when(has_high)
+    def _():
+        to_low.wait_recv()
+
+    @pl.when(band == 0)
+    def _():
+        near[0] = jnp.zeros((8, W), F32)
+
+    @pl.when(band == 15)
+    def _():
+        near[1] = jnp.zeros((8, W), F32)
 
     @pl.when(at_edge)
     def _():
@@ -302,12 +368,19 @@
         turn = 64 - o
         turn = jnp.where(turn < 0, turn + W, turn)
         crossed = pltpu.roll(joined, turn, 1)
-        near[2] = jnp.where(band == 8, crossed, near[2])
-        near[3] = jnp.where(band == 7, crossed, near[3])
-
-    pl.semaphore_wait(met.at[3], len(column))
-
-    image = image_buf[...] - face[2] * near[2] - face[3] * near[3]
+
+        @pl.when(band == 8)
+        def _():
+            near[0] = crossed
+
+        @pl.when(band == 7)
+        def _():
+            near[1] = crossed
+
+
+    pl.semaphore_wait(met.at[2], 1)
+
+    image = image_buf[...] - face[2] * near[0] - face[3] * near[1]
     image_buf[...] = image
 
     late = [jnp.sum(basis[i] * image, axis=0, keepdims=True) for i in range(KB)]
@@ -324,6 +397,8 @@
         some = offsets_of(axes)
         n = len(some)
         src[...] = line
+        if k == 1:
+            pl.semaphore_wait(met.at[3], len(column))
         for s, o in enumerate(some):
             pltpu.make_async_remote_copy(
                 src, slots.at[pl.ds(s, 1), :], ssem, rsem,
@@ -339,8 +414,16 @@
 
     line_out[...] = line
 
-    for copy in halo_copies + near_copies + ends:
+    for copy in [to_left, to_right, edge_left, edge_right] + ends:
         copy.wait_send()
+
+    @pl.when(has_low)
+    def _():
+        to_low.wait_send()
+
+    @pl.when(has_high)
+    def _():
+        to_high.wait_send()
 
     @pl.when(at_edge)
     def _():
@@ -405,16 +488,20 @@
             pltpu.VMEM((2, 320, 640), jnp.bfloat16),
             pltpu.VMEM((8, W), F32),
             pltpu.VMEM((2, 8, W), F32),
+            pltpu.VMEM((2, 8, 640), jnp.bfloat16),
+            pltpu.VMEM((2, 8, 640), jnp.bfloat16),
             pltpu.VMEM((320, 640), jnp.bfloat16),
             pltpu.VMEM((320, 640), jnp.bfloat16),
-            pltpu.VMEM((4, 8, W), F32),
+            pltpu.VMEM((2, 8, W), F32),
             pltpu.VMEM((3, 8, W), F32),
-            pltpu.SemaphoreType.REGULAR((4,)),
+            pltpu.SemaphoreType.REGULAR((5,)),
             dma((14,)),
             dma((2,)),
             dma((2,)),
-            dma((4,)),
-            dma((4,)),
+            dma((2,)),
+            dma((2,)),
+            dma((2,)),
+            dma((2,)),
             dma((3,)),
             dma((3,)),
             *phase_shapes,

time: 47 us -> 44.3 us (0.943)
  Pallas kernels: 45.5 us -> 42.9 us
    pallas_call x1, Pallas kernels: 44.8 us -> 42.2 us  [on_device(): pl.pallas_call(functools.partial(kernel, float(total)), out_shape=(tile,...]
where the time goes in v3:
time: 44.3 us; the launch traced here: 44.2 us
  Pallas kernels  42.9 us (97%)
  between operations  1.29 us (3%)
    pallas_call x1, Pallas kernels, on_device(): pl.pallas_call(functools.partial(kernel, float(total)), out_shape=(tile,...  42.2 us

profile of v3, /device:TPU:1, one launch (start us, length us, event | category | flops | bytes accessed | tf_op | source)
XLA Modules:
  0.0 44.2 jit_solution(14225761782243486716)
XLA Ops:
  1.3 42.2 %schwarz_step.1 = (f32[8,128]{1,0:T(8,128)S(1)}, f32[8,128]{1,0:T(8,128)S(1)}, f32[1,128]{1,0:T(1,128)S(1)}, f32[4,8,128]{2,1,0:T(8,128)S(1)}) custom-call(f32[4,5,1,128]{3,2,1,0:T(1,128)} %basis_hbm.1, f32[5,5,1,128]{3,2,1,0:T(1,128)} %jac_hbm.1, f32[4,5,1,128]{3,2,1,0:T(1,128)} %face_hbm.1, bf16[1,2,320,640]{3,2,1,0:T(8,128)(2,1)} %pinv_hbm.1, s32[1]{0:T(128)S(6)} %copy.8.off), custom_call_target="tpu_custom_call" | custom-call | tf_op jit(solution)/shard_map/schwarz_step/pallas_call | solution.py:475
  43.5 0.7 %schwarz_finish.1 = (f32[5,1,128]{2,1,0:T(1,128)}, f32[5,1,128]{2,1,0:T(1,128)}, f32[5]{0:T(128)}) custom-call(f32[8,128]{1,0:T(8,128)S(1)} %get-tuple-element.7.image, f32[8,128]{1,0:T(8,128)S(1)} %get-tuple-element.8.prec, f32[1,128]{1,0:T(1,128)S(1)} %get-tuple-element.9.line_in, f32[4,8,128]{2,1,0:T(8,128)S(1)} %get-tuple-element.10.basis), custom_call_target="tpu_custom_call" | custom-call | tf_op jit(solution)/shard_map/schwarz_finish/pallas_call | solution.py:514

commit v4 on v3

--- a/solution.py
+++ b/solution.py
@@ -133,6 +133,7 @@
     t0, z, c, y, xl = here
     band = y * 2 + xl
     at_edge = (band == 7) | (band == 8)
+    first = (z == 0) & (c == 0)
     has_low = (band != 0) & (band != 8)
     has_high = (band != 7) & (band != 15)
     left, right = theta_prev(here), theta_next(here)
@@ -188,7 +189,8 @@
 
     @pl.when(band == 8)
     def _():
-        tell(4, opposite3)
+        for k in (1, 0, 2):
+            tell(6 - k, [opposite3[k]])
 
     tell(0, steps)
 
@@ -307,14 +309,22 @@
             )
         )
 
-    @pl.when(band == 7)
-    def _():
-        pl.semaphore_wait(met.at[4], 3)
-
-    @pl.when(at_edge)
-    def _():
-        for copy in rotor_copies:
-            copy.start()
+    def cross(k):
+        @pl.when(band == 7)
+        def _():
+            pl.semaphore_wait(met.at[4 + k], 1)
+
+        rotor_copies[k].start()
+
+    @pl.when(at_edge & first)
+    def _():
+        for k in (1, 2, 0):
+            cross(k)
+
+    @pl.when(at_edge & jnp.logical_not(first))
+    def _():
+        for k in (1, 0, 2):
+            cross(k)
 
     pl.semaphore_wait(met.at[1], len(twos))
     tell(2, [(t0, z, 1 - c, y, xl)])
@@ -494,7 +504,7 @@
             pltpu.VMEM((320, 640), jnp.bfloat16),
             pltpu.VMEM((2, 8, W), F32),
             pltpu.VMEM((3, 8, W), F32),
-            pltpu.SemaphoreType.REGULAR((5,)),
+            pltpu.SemaphoreType.REGULAR((7,)),
             dma((14,)),
             dma((2,)),
             dma((2,)),

time: 44.3 us -> 43.8 us (0.989)
  Pallas kernels: 42.9 us -> 42.3 us
    pallas_call x1, Pallas kernels: 42.2 us -> 41.6 us  [on_device(): pl.pallas_call(functools.partial(kernel, float(total)), out_shape=(tile,...]
where the time goes in v4:
time: 43.8 us; the launch traced here: 43.6 us
  Pallas kernels  42.3 us (97%)
  between operations  1.29 us (3%)
    pallas_call x1, Pallas kernels, on_device(): pl.pallas_call(functools.partial(kernel, float(total)), out_shape=(tile,...  41.6 us

profile of v4, /device:TPU:1, one launch (start us, length us, event | category | flops | bytes accessed | tf_op | source)
XLA Modules:
  0.0 43.6 jit_solution(11161195769741657348)
XLA Ops:
  1.3 41.6 %schwarz_step.1 = (f32[8,128]{1,0:T(8,128)S(1)}, f32[8,128]{1,0:T(8,128)S(1)}, f32[1,128]{1,0:T(1,128)S(1)}, f32[4,8,128]{2,1,0:T(8,128)S(1)}) custom-call(f32[4,5,1,128]{3,2,1,0:T(1,128)} %basis_hbm.1, f32[5,5,1,128]{3,2,1,0:T(1,128)} %jac_hbm.1, f32[4,5,1,128]{3,2,1,0:T(1,128)} %face_hbm.1, bf16[1,2,320,640]{3,2,1,0:T(8,128)(2,1)} %pinv_hbm.1, s32[1]{0:T(128)S(6)} %copy.8.off), custom_call_target="tpu_custom_call" | custom-call | tf_op jit(solution)/shard_map/schwarz_step/pallas_call | solution.py:485
  42.9 0.7 %schwarz_finish.1 = (f32[5,1,128]{2,1,0:T(1,128)}, f32[5,1,128]{2,1,0:T(1,128)}, f32[5]{0:T(128)}) custom-call(f32[8,128]{1,0:T(8,128)S(1)} %get-tuple-element.7.image, f32[8,128]{1,0:T(8,128)S(1)} %get-tuple-element.8.prec, f32[1,128]{1,0:T(1,128)S(1)} %get-tuple-element.9.line_in, f32[4,8,128]{2,1,0:T(8,128)S(1)} %get-tuple-element.10.basis), custom_call_target="tpu_custom_call" | custom-call | tf_op jit(solution)/shard_map/schwarz_finish/pallas_call | solution.py:524

commit v5 on v4

--- a/solution.py
+++ b/solution.py
@@ -109,7 +109,6 @@
     jac,
     face,
     pinv,
-    mine,
     halo,
     edge_out,
     edge_in,
@@ -195,14 +194,12 @@
     tell(0, steps)
 
     copies[KB - 1].wait()
-    own = pltpu.roll(basis[KB - 1].astype(jnp.bfloat16).astype(F32), W // 2, 1)
-    mine[...] = own
 
     to_left = pltpu.make_async_remote_copy(
-        mine, halo.at[1], halo_send.at[0], halo_recv.at[1], device_id=left, device_id_type=MESH
+        basis.at[KB - 1], halo.at[1], halo_send.at[0], halo_recv.at[1], device_id=left, device_id_type=MESH
     )
     to_right = pltpu.make_async_remote_copy(
-        mine, halo.at[0], halo_send.at[1], halo_recv.at[0], device_id=right, device_id_type=MESH
+        basis.at[KB - 1], halo.at[0], halo_send.at[1], halo_recv.at[0], device_id=right, device_id_type=MESH
     )
     edge_left = pltpu.make_async_remote_copy(
         edge_out.at[0], edge_in.at[1], edge_send.at[0], edge_recv.at[1],
@@ -215,6 +212,8 @@
     to_right.start()
 
     to_left.start()
+
+    own = pltpu.roll(basis[KB - 1].astype(jnp.bfloat16).astype(F32), W // 2, 1)
 
     pinv_copy.wait()
 
@@ -279,7 +278,8 @@
 
     to_right.wait_recv()
     to_left.wait_recv()
-    ph = jnp.where(lane < W // 2, halo[0], halo[1])
+    ph = jnp.where(lane < W // 2, halo[1], halo[0]).astype(jnp.bfloat16).astype(F32)
+    ph = pltpu.roll(ph, W // 2, 1)
     halo_part = fold(times(bhalo[...], spread(ph, same)))
     zero1 = jnp.zeros((1, W), F32)
     pre = jnp.concatenate([a + b for a, b in zip(own_part, halo_part)] + [zero1] * 3, axis=0)
@@ -496,7 +496,6 @@
             pltpu.VMEM((NC, 8, W), F32),
             pltpu.VMEM((4, 8, W), F32),
             pltpu.VMEM((2, 320, 640), jnp.bfloat16),
-            pltpu.VMEM((8, W), F32),
             pltpu.VMEM((2, 8, W), F32),
             pltpu.VMEM((2, 8, 640), jnp.bfloat16),
             pltpu.VMEM((2, 8, 640), jnp.bfloat16),

time: 43.8 us -> 43.8 us (level)
  no operation moved by 1% of the time
where the time goes in v5:
time: 43.8 us; the launch traced here: 43.6 us
  Pallas kernels  42.3 us (97%)
  between operations  1.29 us (3%)
    pallas_call x1, Pallas kernels, on_device(): pl.pallas_call(functools.partial(kernel, float(total)), out_shape=(tile,...  41.6 us

profile of v5, /device:TPU:1, one launch (start us, length us, event | category | flops | bytes accessed | tf_op | source)
XLA Modules:
  0.0 43.6 jit_solution(14938162609223561024)
XLA Ops:
  1.3 41.6 %schwarz_step.1 = (f32[8,128]{1,0:T(8,128)S(1)}, f32[8,128]{1,0:T(8,128)S(1)}, f32[1,128]{1,0:T(1,128)S(1)}, f32[4,8,128]{2,1,0:T(8,128)S(1)}) custom-call(f32[4,5,1,128]{3,2,1,0:T(1,128)} %basis_hbm.1, f32[5,5,1,128]{3,2,1,0:T(1,128)} %jac_hbm.1, f32[4,5,1,128]{3,2,1,0:T(1,128)} %face_hbm.1, bf16[1,2,320,640]{3,2,1,0:T(8,128)(2,1)} %pinv_hbm.1, s32[1]{0:T(128)S(6)} %copy.8.off), custom_call_target="tpu_custom_call" | custom-call | tf_op jit(solution)/shard_map/schwarz_step/pallas_call | solution.py:485
  42.9 0.7 %schwarz_finish.1 = (f32[5,1,128]{2,1,0:T(1,128)}, f32[5,1,128]{2,1,0:T(1,128)}, f32[5]{0:T(128)}) custom-call(f32[8,128]{1,0:T(8,128)S(1)} %get-tuple-element.7.image, f32[8,128]{1,0:T(8,128)S(1)} %get-tuple-element.8.prec, f32[1,128]{1,0:T(1,128)S(1)} %get-tuple-element.9.line_in, f32[4,8,128]{2,1,0:T(8,128)S(1)} %get-tuple-element.10.basis), custom_call_target="tpu_custom_call" | custom-call | tf_op jit(solution)/shard_map/schwarz_finish/pallas_call | solution.py:523
